TPU v7x, 128 devices: a whole 4x4x4 slice. The times are simulated.
128 devices in a mesh: py: 4 (over y), px: 4 (over z), pz: 8 (over x, core).
Axes of the slice: x: 4, y: 4, z: 4, core: 2. Of those that a mesh axis runs over, the one named last changes fastest.
Arguments:
- field_now: float32 [16, 512, 256, 128], P('py', 'px', 'pz'), may hold values from 0.5 to 2
- earlier: float32 [16, 512, 256, 128], P('py', 'px', 'pz'), may hold values from 0.2 to 1.8
- speed_square: float32 [16, 512, 256, 128], P('py', 'px', 'pz'), may hold values from 0.05 to 0.3
Outputs:
- anomaly: float32 [16, 512, 256, 128], P('py', 'px', 'pz')
- field_now_end: float32 [16, 512, 256, 128], P('py', 'px', 'pz')
All inputs are finite; a program needn't handle non-finite values.
Results may differ from a plain program's by a relative error of at most 0.00002.
Values sent between devices are 32-bit elements; how exact they have to be, the bound alone decides.
A program may use at most 128 MiB of HBM per device.

v0:
```python
import jax
import jax.numpy as jnp
from jax import lax
from jax.sharding import PartitionSpec as P

STEPS = 4


def with_halo(array, sides, width):
    edges = {}
    for axis, dim in sides:
        devices, length = (lax.axis_size(axis), array.shape[dim])
        up = [(i, (i + 1) % devices) for i in range(devices - 1)]
        last = lax.slice_in_dim(array, length - width, length, axis=dim)
        leading = lax.slice_in_dim(array, 0, width, axis=dim)
        edges[dim] = (
            lax.ppermute(last, axis, up),
            lax.ppermute(leading, axis, [(b, a) for a, b in up]),
        )
    done = []
    for _, dim in sides:
        low, high = edges[dim]
        around = [(width, width) if d in done else (0, 0) for d in range(array.ndim)]
        array = jnp.concatenate([jnp.pad(low, around), array, jnp.pad(high, around)], axis=dim)
        done.append(dim)
    return array


def copy_for_each(array, axis):
    devices = lax.axis_size(axis)
    return lax.all_to_all(
        jnp.broadcast_to(array[None], (devices, *array.shape)), axis, 0, 0, tiled=True
    )


def of_everyone(array, axis):
    everything = copy_for_each(array, axis)
    return jnp.sum(everything, axis=0)


def packed_total(arrays, axis):
    ends = [0]
    for a in arrays:
        ends.append(ends[-1] + a.size)
    so_far = of_everyone(jnp.concatenate([a.ravel() for a in arrays]), axis)
    return tuple((so_far[b:e].reshape(a.shape) for a, b, e in zip(arrays, ends, ends[1:])))


def inner_cells(values, dims):
    for dim in dims:
        values = lax.slice_in_dim(values, 1, values.shape[dim] - 1, axis=dim)
    return values


def side_cells(values, dim, start, dims):
    others = [other for other in dims if other != dim]
    values = inner_cells(values, others)
    return lax.slice_in_dim(values, start, start + values.shape[dim] - 2, axis=dim)


def advance(padded, before, speed_square):
    middle = inner_cells(padded, (0, 1, 2))
    lower = [side_cells(padded, dim, 0, (0, 1, 2)) for dim in (0, 1, 2)]
    upper = [side_cells(padded, dim, 2, (0, 1, 2)) for dim in (0, 1, 2)]
    spread = lower[0] + upper[0] + lower[1] + upper[1] + lower[2] + upper[2] - 6.0 * middle
    return 2.0 * middle - before + speed_square * spread


def shards(field_now, earlier, speed_square):
    for step in range(STEPS):
        padded = with_halo(field_now, (("py", 0), ("px", 1), ("pz", 2)), 1)
        later = advance(padded, earlier, speed_square)
        earlier, field_now = (field_now, later)
    count = field_now.shape[1] * lax.axis_size("px")
    guess = 1.0
    moved = field_now - guess
    totals, squares = packed_total(
        (jnp.sum(moved, axis=1, keepdims=True), jnp.sum(moved * moved, axis=1, keepdims=True)), "px"
    )
    line_mean = guess + totals / count
    centred = field_now - line_mean
    line_variance = squares / count - totals / count * (totals / count)
    anomaly = centred * lax.rsqrt(line_variance + 0.0001)
    return (anomaly, field_now)


def solution(mesh):
    return jax.shard_map(
        shards,
        mesh=mesh,
        in_specs=(P("py", "px", "pz", None), P("py", "px", "pz", None), P("py", "px", "pz", None)),
        out_specs=(P("py", "px", "pz", None), P("py", "px", "pz", None)),
        check_vma=False,
    )
```

profile of v0, /device:TPU:0, one launch (start us, length us, event | category | flops | bytes accessed | tf_op | source)
XLA Modules:
  0.0 378.7 jit_solution(15956215428659775308)
XLA Ops:
  0.6 8.2 %copy.43 = f32[4,128,32,128]{3,1,2,0:T(8,128)S(1)} copy(f32[4,128,32,128]{3,2,1,0:T(8,128)} %param.3) | data formatting | bytes 16777216 | tf_op args[0]
  10.6 4.1 %collective-permute-start = (f32[1,128,32,128]{3,1,2,0:T(8,128)S(1)}, f32[1,128,32,128]{3,1,2,0:T(8,128)S(1)}, u32[]{:S(2)}, u32[]{:S(2)}) collective-permute-start(f32[1,128,32,128]{3,1,2,0:T(8,128)S(1)} %get-tuple-element.34), channel_id=1, source_target_pairs={{0,32},{32,64},{64,96},{1,33},{33,65},{65,97},{2,34},{34,66},{66,9... | collective-permute-start | bytes 6291464 | tf_op jit(solution)/shard_map/ppermute | solution.py:17
  16.2 3.8 %collective-permute-start.2 = (f32[4,1,32,128]{3,1,2,0:T(1,128)S(1)}, f32[4,1,32,128]{3,1,2,0:T(1,128)S(1)}, u32[]{:S(2)}, u32[]{:S(2)}) collective-permute-start(f32[4,1,32,128]{3,1,2,0:T(1,128)S(1)} %bitcast.13), channel_id=1, source_target_pairs={{0,8},{8,16},{16,24},{1,9},{9,17},{17,25},{2,10},{10,18},{18,26},{... | collective-permute-start | bytes 196616 | tf_op jit(solution)/shard_map/ppermute | solution.py:17
  26.2 33.2 %collective-permute-done = f32[1,128,32,128]{3,1,2,0:T(8,128)S(1)} collective-permute-done((f32[1,128,32,128]{3,1,2,0:T(8,128)S(1)}, f32[1,128,32,128]{3,1,2,0:T(8,128)S(1)}, u32[]{:S(2)}, u32[]{:S(2)}) %collective-permute-start) | collective-permute-done | bytes 2097184 | tf_op jit(solution)/shard_map/ppermute | solution.py:17
  60.9 8.2 %constant_dynamic-update-slice_fusion.1 = f32[6,128,32,128]{3,1,2,0:T(8,128)} fusion(f32[6,128,32,128]{3,1,2,0:T(8,128)} %constant_dynamic-update-slice_fusion.2, f32[4,128,32,128]{3,2,1,0:T(8,128)S(1)} %copy-done), kind=kLoop, calls=%fused_computation.118 | loop fusion | bytes 16777216
  72.4 27.4 %fusion.34 = f32[4,128,32,128]{3,1,2,0:T(8,128)} fusion(f32[4,128,1,128]{3,1,2,0:T(8,128)S(1)} %collective-permute-done.5, f32[6,1,32,128]{3,1,2,0:T(1,128)S(1)} %pad.51, f32[6,128,32,128]{3,1,2,0:T(8,128)} %constant_dynamic-update-slice_fusion, f32[6,1,32,128]{3,1,2,0:T(1,128)S(1)} %pad.50, f32[4,128,1,128]{3,1,2,0:T(8,128)S(1)} %collective-permute-done.4, ...), kind=kLoop, calls=%fused_computation.89 | loop fusion | flops 56623104 | bytes 51052544 | tf_op jit(solution)/shard_map/add | solution.py:66
  102.3 4.5 %collective-permute-start.6 = (f32[1,128,32,128]{3,1,2,0:T(8,128)S(1)}, f32[1,128,32,128]{3,1,2,0:T(8,128)S(1)}, u32[]{:S(2)}, u32[]{:S(2)}) collective-permute-start(f32[1,128,32,128]{3,1,2,0:T(8,128)S(1)} %get-tuple-element.25), channel_id=1, source_target_pairs={{0,32},{32,64},{64,96},{1,33},{33,65},{65,97},{2,34},{34,66},{66,9... | collective-permute-start | bytes 6291464 | tf_op jit(solution)/shard_map/ppermute | solution.py:17
  113.1 3.8 %collective-permute-start.8 = (f32[4,1,32,128]{3,1,2,0:T(1,128)S(1)}, f32[4,1,32,128]{3,1,2,0:T(1,128)S(1)}, u32[]{:S(2)}, u32[]{:S(2)}) collective-permute-start(f32[4,1,32,128]{3,1,2,0:T(1,128)S(1)} %get-tuple-element.27), channel_id=1, source_target_pairs={{0,8},{8,16},{16,24},{1,9},{9,17},{17,25},{2,10},{10,18},{18,26},{... | collective-permute-start | bytes 196616 | tf_op jit(solution)/shard_map/ppermute | solution.py:17
  120.4 4.9 %collective-permute-done.9 = f32[4,1,32,128]{3,1,2,0:T(1,128)S(1)} collective-permute-done((f32[4,1,32,128]{3,1,2,0:T(1,128)S(1)}, f32[4,1,32,128]{3,1,2,0:T(1,128)S(1)}, u32[]{:S(2)}, u32[]{:S(2)}) %collective-permute-start.9) | collective-permute-done | bytes 65568 | tf_op jit(solution)/shard_map/ppermute | solution.py:18
  125.4 25.4 %collective-permute-done.6 = f32[1,128,32,128]{3,1,2,0:T(8,128)S(1)} collective-permute-done((f32[1,128,32,128]{3,1,2,0:T(8,128)S(1)}, f32[1,128,32,128]{3,1,2,0:T(8,128)S(1)}, u32[]{:S(2)}, u32[]{:S(2)}) %collective-permute-start.6) | collective-permute-done | bytes 2097184 | tf_op jit(solution)/shard_map/ppermute | solution.py:17
  150.8 4.4 %collective-permute-done.7 = f32[1,128,32,128]{3,1,2,0:T(8,128)} collective-permute-done((f32[1,128,32,128]{3,1,2,0:T(8,128)S(1)}, f32[1,128,32,128]{3,1,2,0:T(8,128)}, u32[]{:S(2)}, u32[]{:S(2)}) %collective-permute-start.7) | collective-permute-done | bytes 2097184 | tf_op jit(solution)/shard_map/ppermute | solution.py:18
  155.2 28.9 %fusion.24 = f32[4,128,32,128]{3,1,2,0:T(8,128)} fusion(f32[4,128,1,128]{3,1,2,0:T(8,128)S(1)} %collective-permute-done.11, f32[6,1,32,128]{3,1,2,0:T(1,128)S(1)} %pad.55, f32[6,1,32,128]{3,1,2,0:T(1,128)S(1)} %pad.54, f32[1,128,32,128]{3,1,2,0:T(8,128)} %collective-permute-done.7, f32[4,128,32,128]{3,1,2,0:T(8,128)} %fusion.34, ...), kind=kLoop, calls=%fused_computation.61 | loop fusion | flops 73400320 | bytes 38469632 | tf_op jit(solution)/shard_map/add | solution.py:66
  203.4 5.1 %collective-permute-done.15 = f32[4,1,32,128]{3,1,2,0:T(1,128)S(1)} collective-permute-done((f32[4,1,32,128]{3,1,2,0:T(1,128)S(1)}, f32[4,1,32,128]{3,1,2,0:T(1,128)S(1)}, u32[]{:S(2)}, u32[]{:S(2)}) %collective-permute-start.15) | collective-permute-done | bytes 65568 | tf_op jit(solution)/shard_map/ppermute | solution.py:18
  208.6 24.3 %collective-permute-done.12 = f32[1,128,32,128]{3,1,2,0:T(8,128)S(1)} collective-permute-done((f32[1,128,32,128]{3,1,2,0:T(8,128)S(1)}, f32[1,128,32,128]{3,1,2,0:T(8,128)S(1)}, u32[]{:S(2)}, u32[]{:S(2)}) %collective-permute-start.12) | collective-permute-done | bytes 2097184 | tf_op jit(solution)/shard_map/ppermute | solution.py:17
  232.9 4.4 %collective-permute-done.13 = f32[1,128,32,128]{3,1,2,0:T(8,128)} collective-permute-done((f32[1,128,32,128]{3,1,2,0:T(8,128)S(1)}, f32[1,128,32,128]{3,1,2,0:T(8,128)}, u32[]{:S(2)}, u32[]{:S(2)}) %collective-permute-start.13) | collective-permute-done | bytes 2097184 | tf_op jit(solution)/shard_map/ppermute | solution.py:18
  237.2 28.5 %fusion.14 = f32[4,128,32,128]{3,1,2,0:T(8,128)} fusion(f32[4,128,1,128]{3,1,2,0:T(8,128)S(1)} %collective-permute-done.17, f32[6,1,32,128]{3,1,2,0:T(1,128)S(1)} %pad.59, f32[6,1,32,128]{3,1,2,0:T(1,128)S(1)} %pad.58, f32[1,128,32,128]{3,1,2,0:T(8,128)} %collective-permute-done.13, f32[4,128,32,128]{3,1,2,0:T(8,128)} %fusion.24, ...), kind=kLoop, calls=%fused_computation.33 | loop fusion | flops 73400320 | bytes 38469632 | tf_op jit(solution)/shard_map/add | solution.py:66
  284.6 5.1 %collective-permute-done.21 = f32[4,1,32,128]{3,1,2,0:T(1,128)S(1)} collective-permute-done((f32[4,1,32,128]{3,1,2,0:T(1,128)S(1)}, f32[4,1,32,128]{3,1,2,0:T(1,128)S(1)}, u32[]{:S(2)}, u32[]{:S(2)}) %collective-permute-start.21) | collective-permute-done | bytes 65568 | tf_op jit(solution)/shard_map/ppermute | solution.py:18
  289.8 23.0 %collective-permute-done.18 = f32[1,128,32,128]{3,1,2,0:T(8,128)S(1)} collective-permute-done((f32[1,128,32,128]{3,1,2,0:T(8,128)S(1)}, f32[1,128,32,128]{3,1,2,0:T(8,128)S(1)}, u32[]{:S(2)}, u32[]{:S(2)}) %collective-permute-start.18) | collective-permute-done | bytes 2097184 | tf_op jit(solution)/shard_map/ppermute | solution.py:17
  312.9 4.4 %collective-permute-done.19 = f32[1,128,32,128]{3,1,2,0:T(8,128)} collective-permute-done((f32[1,128,32,128]{3,1,2,0:T(8,128)S(1)}, f32[1,128,32,128]{3,1,2,0:T(8,128)}, u32[]{:S(2)}, u32[]{:S(2)}) %collective-permute-start.19) | collective-permute-done | bytes 2097184 | tf_op jit(solution)/shard_map/ppermute | solution.py:18
  317.2 29.0 %add_reduce_fusion = (f32[4,32,128]{2,1,0:T(8,128)S(1)}, f32[4,32,128]{2,1,0:T(8,128)S(1)}, f32[4,128,32,128]{3,1,2,0:T(8,128)}) fusion(f32[4,128,32,128]{3,1,2,0:T(8,128)} %fusion.14, f32[4,128,1,128]{3,1,2,0:T(8,128)S(1)} %collective-permute-done.23, f32[6,1,32,128]{3,1,2,0:T(1,128)S(1)} %pad.63, f32[1,128,32,128]{3,1,2,0:T(8,128)} %collective-permute-done.19, ...), kind=kLoop, calls=%fused_computation.109 | loop fusion | flops 81756160 | bytes 38600704 | tf_op jit(solution)/shard_map/reduce_sum | solution.py:78
  347.3 5.5 %all-to-all-start = ((f32[4,1,32768]{2,1,0:T(1,128)}), f32[4,1,32768]{2,1,0:T(1,128)S(1)}, u32[]{:S(2)}, u32[]{:S(2)}) async-start(f32[4,1,32768]{2,1,0:T(1,128)} %broadcast_in_dim.2), calls=%async_computation | async-start | bytes 1048576 | tf_op jit(solution)/shard_map/all_to_all | solution.py:31
  352.9 11.6 %copy.62 = f32[4,128,32,128]{3,2,1,0:T(8,128)} copy(f32[4,128,32,128]{3,1,2,0:T(8,128)} %get-tuple-element.10) | data formatting | bytes 16777216
  365.0 5.0 %subtract_multiply_fusion = f32[4,128,32,128]{3,1,2,0:T(8,128)S(1)} fusion(f32[4,128,32,128]{3,1,2,0:T(8,128)} %get-tuple-element.10, f32[4,32,128]{2,1,0:T(8,128)S(1)} %bitcast.11, f32[4,32,128]{2,1,0:T(8,128)S(1)} %bitcast.10), kind=kLoop, calls=%fused_computation.107 | loop fusion | flops 4194304 | bytes 16908288 | tf_op jit(solution)/shard_map/mul | solution.py:83
  370.0 8.3 %copy.61 = f32[4,128,32,128]{3,2,1,0:T(8,128)} copy(f32[4,128,32,128]{3,1,2,0:T(8,128)S(1)} %subtract_multiply_fusion) | data formatting | bytes 16777216
  (70 shorter events, 66.1 us)
Async XLA Ops:
  10.6 48.9 %collective-permute-start = (f32[1,128,32,128]{3,1,2,0:T(8,128)S(1)}, f32[1,128,32,128]{3,1,2,0:T(8,128)S(1)}, u32[]{:S(2)}, u32[]{:S(2)}) collective-permute-start(f32[1,128,32,128]{3,1,2,0:T(8,128)S(1)} %get-tuple-element.34), channel_id=1, source_target_pairs={{0,32},{32,64},{64,96},{1,33},{33,65},{65,97},{2,34},{34,66},{66,9... | collective-permute-start | bytes 6291464 | tf_op jit(solution)/shard_map/ppermute | solution.py:17
  14.7 54.5 %collective-permute-start.1 = (f32[1,128,32,128]{3,1,2,0:T(8,128)}, f32[1,128,32,128]{3,1,2,0:T(8,128)}, u32[]{:S(2)}, u32[]{:S(2)}) collective-permute-start(f32[1,128,32,128]{3,1,2,0:T(8,128)} %get-tuple-element.33), channel_id=1, source_target_pairs={{32,0},{64,32},{96,64},{33,1},{65,33},{97,65},{34,2},{66,34},{98,6... | collective-permute-start | bytes 6291464 | tf_op jit(solution)/shard_map/ppermute | solution.py:18
  16.2 7.3 %collective-permute-start.2 = (f32[4,1,32,128]{3,1,2,0:T(1,128)S(1)}, f32[4,1,32,128]{3,1,2,0:T(1,128)S(1)}, u32[]{:S(2)}, u32[]{:S(2)}) collective-permute-start(f32[4,1,32,128]{3,1,2,0:T(1,128)S(1)} %bitcast.13), channel_id=1, source_target_pairs={{0,8},{8,16},{16,24},{1,9},{9,17},{17,25},{2,10},{10,18},{18,26},{... | collective-permute-start | bytes 196616 | tf_op jit(solution)/shard_map/ppermute | solution.py:17
  20.0 6.2 %collective-permute-start.3 = (f32[4,1,32,128]{3,1,2,0:T(1,128)S(1)}, f32[4,1,32,128]{3,1,2,0:T(1,128)S(1)}, u32[]{:S(2)}, u32[]{:S(2)}) collective-permute-start(f32[4,1,32,128]{3,1,2,0:T(1,128)S(1)} %bitcast.12), channel_id=1, source_target_pairs={{8,0},{16,8},{24,16},{9,1},{17,9},{25,17},{10,2},{18,10},{26,18},{... | collective-permute-start | bytes 196616 | tf_op jit(solution)/shard_map/ppermute | solution.py:18
  22.0 50.3 %collective-permute-start.4 = (f32[4,128,1,128]{3,1,2,0:T(8,128)}, f32[4,128,1,128]{3,1,2,0:T(8,128)S(1)}, u32[]{:S(2)}, u32[]{:S(2)}) collective-permute-start(f32[4,128,1,128]{3,1,2,0:T(8,128)} %get-tuple-element.29), channel_id=1, source_target_pairs={{0,1},{1,2},{2,3},{3,4},{4,5},{5,6},{6,7},{8,9},{9,10},{10,11},{11... | collective-permute-start | bytes 786440 | tf_op jit(solution)/shard_map/ppermute | solution.py:17
  23.5 48.9 %collective-permute-start.5 = (f32[4,128,1,128]{3,1,2,0:T(8,128)S(1)}, f32[4,128,1,128]{3,1,2,0:T(8,128)S(1)}, u32[]{:S(2)}, u32[]{:S(2)}) collective-permute-start(f32[4,128,1,128]{3,1,2,0:T(8,128)S(1)} %get-tuple-element.30), channel_id=1, source_target_pairs={{1,0},{2,1},{3,2},{4,3},{5,4},{6,5},{7,6},{9,8},{10,9},{11,10},{12... | collective-permute-start | bytes 786440 | tf_op jit(solution)/shard_map/ppermute | solution.py:18
  102.3 48.5 %collective-permute-start.6 = (f32[1,128,32,128]{3,1,2,0:T(8,128)S(1)}, f32[1,128,32,128]{3,1,2,0:T(8,128)S(1)}, u32[]{:S(2)}, u32[]{:S(2)}) collective-permute-start(f32[1,128,32,128]{3,1,2,0:T(8,128)S(1)} %get-tuple-element.25), channel_id=1, source_target_pairs={{0,32},{32,64},{64,96},{1,33},{33,65},{65,97},{2,34},{34,66},{66,9... | collective-permute-start | bytes 6291464 | tf_op jit(solution)/shard_map/ppermute | solution.py:17
  106.8 48.3 %collective-permute-start.7 = (f32[1,128,32,128]{3,1,2,0:T(8,128)S(1)}, f32[1,128,32,128]{3,1,2,0:T(8,128)}, u32[]{:S(2)}, u32[]{:S(2)}) collective-permute-start(f32[1,128,32,128]{3,1,2,0:T(8,128)S(1)} %get-tuple-element.26), channel_id=1, source_target_pairs={{32,0},{64,32},{96,64},{33,1},{65,33},{97,65},{34,2},{66,34},{98,6... | collective-permute-start | bytes 6291464 | tf_op jit(solution)/shard_map/ppermute | solution.py:18
  109.2 16.2 %collective-permute-start.10 = (f32[4,128,1,128]{3,1,2,0:T(8,128)S(1)}, f32[4,128,1,128]{3,1,2,0:T(8,128)S(1)}, u32[]{:S(2)}, u32[]{:S(2)}) collective-permute-start(f32[4,128,1,128]{3,1,2,0:T(8,128)S(1)} %get-tuple-element.23), channel_id=1, source_target_pairs={{0,1},{1,2},{2,3},{3,4},{4,5},{5,6},{6,7},{8,9},{9,10},{10,11},{11... | collective-permute-start | bytes 786440 | tf_op jit(solution)/shard_map/ppermute | solution.py:17
  110.5 14.9 %collective-permute-start.11 = (f32[4,128,1,128]{3,1,2,0:T(8,128)S(1)}, f32[4,128,1,128]{3,1,2,0:T(8,128)S(1)}, u32[]{:S(2)}, u32[]{:S(2)}) collective-permute-start(f32[4,128,1,128]{3,1,2,0:T(8,128)S(1)} %get-tuple-element.24), channel_id=1, source_target_pairs={{1,0},{2,1},{3,2},{4,3},{5,4},{6,5},{7,6},{9,8},{10,9},{11,10},{12... | collective-permute-start | bytes 786440 | tf_op jit(solution)/shard_map/ppermute | solution.py:18
  113.1 5.7 %collective-permute-start.8 = (f32[4,1,32,128]{3,1,2,0:T(1,128)S(1)}, f32[4,1,32,128]{3,1,2,0:T(1,128)S(1)}, u32[]{:S(2)}, u32[]{:S(2)}) collective-permute-start(f32[4,1,32,128]{3,1,2,0:T(1,128)S(1)} %get-tuple-element.27), channel_id=1, source_target_pairs={{0,8},{8,16},{16,24},{1,9},{9,17},{17,25},{2,10},{10,18},{18,26},{... | collective-permute-start | bytes 196616 | tf_op jit(solution)/shard_map/ppermute | solution.py:17
  118.8 6.5 %collective-permute-start.9 = (f32[4,1,32,128]{3,1,2,0:T(1,128)S(1)}, f32[4,1,32,128]{3,1,2,0:T(1,128)S(1)}, u32[]{:S(2)}, u32[]{:S(2)}) collective-permute-start(f32[4,1,32,128]{3,1,2,0:T(1,128)S(1)} %get-tuple-element.28), channel_id=1, source_target_pairs={{8,0},{16,8},{24,16},{9,1},{17,9},{25,17},{10,2},{18,10},{26,18},{... | collective-permute-start | bytes 196616 | tf_op jit(solution)/shard_map/ppermute | solution.py:18
  186.5 46.3 %collective-permute-start.12 = (f32[1,128,32,128]{3,1,2,0:T(8,128)S(1)}, f32[1,128,32,128]{3,1,2,0:T(8,128)S(1)}, u32[]{:S(2)}, u32[]{:S(2)}) collective-permute-start(f32[1,128,32,128]{3,1,2,0:T(8,128)S(1)} %get-tuple-element.19), channel_id=1, source_target_pairs={{0,32},{32,64},{64,96},{1,33},{33,65},{65,97},{2,34},{34,66},{66,9... | collective-permute-start | bytes 6291464 | tf_op jit(solution)/shard_map/ppermute | solution.py:17
  190.0 47.2 %collective-permute-start.13 = (f32[1,128,32,128]{3,1,2,0:T(8,128)S(1)}, f32[1,128,32,128]{3,1,2,0:T(8,128)}, u32[]{:S(2)}, u32[]{:S(2)}) collective-permute-start(f32[1,128,32,128]{3,1,2,0:T(8,128)S(1)} %get-tuple-element.20), channel_id=1, source_target_pairs={{32,0},{64,32},{96,64},{33,1},{65,33},{97,65},{34,2},{66,34},{98,6... | collective-permute-start | bytes 6291464 | tf_op jit(solution)/shard_map/ppermute | solution.py:18
  192.4 16.2 %collective-permute-start.16 = (f32[4,128,1,128]{3,1,2,0:T(8,128)S(1)}, f32[4,128,1,128]{3,1,2,0:T(8,128)S(1)}, u32[]{:S(2)}, u32[]{:S(2)}) collective-permute-start(f32[4,128,1,128]{3,1,2,0:T(8,128)S(1)} %get-tuple-element.17), channel_id=1, source_target_pairs={{0,1},{1,2},{2,3},{3,4},{4,5},{5,6},{6,7},{8,9},{9,10},{10,11},{11... | collective-permute-start | bytes 786440 | tf_op jit(solution)/shard_map/ppermute | solution.py:17
  193.7 14.9 %collective-permute-start.17 = (f32[4,128,1,128]{3,1,2,0:T(8,128)S(1)}, f32[4,128,1,128]{3,1,2,0:T(8,128)S(1)}, u32[]{:S(2)}, u32[]{:S(2)}) collective-permute-start(f32[4,128,1,128]{3,1,2,0:T(8,128)S(1)} %get-tuple-element.18), channel_id=1, source_target_pairs={{1,0},{2,1},{3,2},{4,3},{5,4},{6,5},{7,6},{9,8},{10,9},{11,10},{12... | collective-permute-start | bytes 786440 | tf_op jit(solution)/shard_map/ppermute | solution.py:18
  202.0 6.5 %collective-permute-start.15 = (f32[4,1,32,128]{3,1,2,0:T(1,128)S(1)}, f32[4,1,32,128]{3,1,2,0:T(1,128)S(1)}, u32[]{:S(2)}, u32[]{:S(2)}) collective-permute-start(f32[4,1,32,128]{3,1,2,0:T(1,128)S(1)} %get-tuple-element.22), channel_id=1, source_target_pairs={{8,0},{16,8},{24,16},{9,1},{17,9},{25,17},{10,2},{18,10},{26,18},{... | collective-permute-start | bytes 196616 | tf_op jit(solution)/shard_map/ppermute | solution.py:18
  268.3 44.6 %collective-permute-start.18 = (f32[1,128,32,128]{3,1,2,0:T(8,128)S(1)}, f32[1,128,32,128]{3,1,2,0:T(8,128)S(1)}, u32[]{:S(2)}, u32[]{:S(2)}) collective-permute-start(f32[1,128,32,128]{3,1,2,0:T(8,128)S(1)} %get-tuple-element.15), channel_id=1, source_target_pairs={{0,32},{32,64},{64,96},{1,33},{33,65},{65,97},{2,34},{34,66},{66,9... | collective-permute-start | bytes 6291464 | tf_op jit(solution)/shard_map/ppermute | solution.py:17
  271.2 46.0 %collective-permute-start.19 = (f32[1,128,32,128]{3,1,2,0:T(8,128)S(1)}, f32[1,128,32,128]{3,1,2,0:T(8,128)}, u32[]{:S(2)}, u32[]{:S(2)}) collective-permute-start(f32[1,128,32,128]{3,1,2,0:T(8,128)S(1)} %get-tuple-element.16), channel_id=1, source_target_pairs={{32,0},{64,32},{96,64},{33,1},{65,33},{97,65},{34,2},{66,34},{98,6... | collective-permute-start | bytes 6291464 | tf_op jit(solution)/shard_map/ppermute | solution.py:18
  273.6 16.2 %collective-permute-start.22 = (f32[4,128,1,128]{3,1,2,0:T(8,128)S(1)}, f32[4,128,1,128]{3,1,2,0:T(8,128)S(1)}, u32[]{:S(2)}, u32[]{:S(2)}) collective-permute-start(f32[4,128,1,128]{3,1,2,0:T(8,128)S(1)} %get-tuple-element.11), channel_id=1, source_target_pairs={{0,1},{1,2},{2,3},{3,4},{4,5},{5,6},{6,7},{8,9},{9,10},{10,11},{11... | collective-permute-start | bytes 786440 | tf_op jit(solution)/shard_map/ppermute | solution.py:17
  274.9 14.9 %collective-permute-start.23 = (f32[4,128,1,128]{3,1,2,0:T(8,128)S(1)}, f32[4,128,1,128]{3,1,2,0:T(8,128)S(1)}, u32[]{:S(2)}, u32[]{:S(2)}) collective-permute-start(f32[4,128,1,128]{3,1,2,0:T(8,128)S(1)} %get-tuple-element.12), channel_id=1, source_target_pairs={{1,0},{2,1},{3,2},{4,3},{5,4},{6,5},{7,6},{9,8},{10,9},{11,10},{12... | collective-permute-start | bytes 786440 | tf_op jit(solution)/shard_map/ppermute | solution.py:18
  277.5 5.7 %collective-permute-start.20 = (f32[4,1,32,128]{3,1,2,0:T(1,128)S(1)}, f32[4,1,32,128]{3,1,2,0:T(1,128)S(1)}, u32[]{:S(2)}, u32[]{:S(2)}) collective-permute-start(f32[4,1,32,128]{3,1,2,0:T(1,128)S(1)} %get-tuple-element.13), channel_id=1, source_target_pairs={{0,8},{8,16},{16,24},{1,9},{9,17},{17,25},{2,10},{10,18},{18,26},{... | collective-permute-start | bytes 196616 | tf_op jit(solution)/shard_map/ppermute | solution.py:17
  283.3 6.5 %collective-permute-start.21 = (f32[4,1,32,128]{3,1,2,0:T(1,128)S(1)}, f32[4,1,32,128]{3,1,2,0:T(1,128)S(1)}, u32[]{:S(2)}, u32[]{:S(2)}) collective-permute-start(f32[4,1,32,128]{3,1,2,0:T(1,128)S(1)} %get-tuple-element.14), channel_id=1, source_target_pairs={{8,0},{16,8},{24,16},{9,1},{17,9},{25,17},{10,2},{18,10},{26,18},{... | collective-permute-start | bytes 196616 | tf_op jit(solution)/shard_map/ppermute | solution.py:18
  347.3 17.2 %all-to-all-start = ((f32[4,1,32768]{2,1,0:T(1,128)}), f32[4,1,32768]{2,1,0:T(1,128)S(1)}, u32[]{:S(2)}, u32[]{:S(2)}) async-start(f32[4,1,32768]{2,1,0:T(1,128)} %broadcast_in_dim.2), calls=%async_computation | async-start | bytes 1048576 | tf_op jit(solution)/shard_map/all_to_all | solution.py:31
  (5 other events, 54.7 us)
where the time goes:
time: 384 us; the launch traced here: 379 us
  waiting for transfers between devices  141 us (37%)
  other arithmetic  119 us (31%)
  local copies, waits for them, and re-layouts  59.7 us (16%)
  starting transfers between devices  57.2 us (15%)
    ppermute x12, waiting for transfers between devices, with_halo(): lax.ppermute(last, axis, up)  112 us
    add x3, other arithmetic, advance(): return 2.0 * middle - before + speed_square * spread  84.8 us
    unnamed x13, local copies, waits for them, and re-layouts  37.9 us
    ppermute x12, starting transfers between devices, with_halo(): lax.ppermute(last, axis, up)  35.7 us
    ppermute x12, waiting for transfers between devices, with_halo(): lax.ppermute(leading, axis, [(b, a) for a, b in up])  29.4 us
    reduce_sum x1, other arithmetic, shards(): jnp.sum(moved, axis=1, keepdims=True)  29 us
    ppermute x12, starting transfers between devices, with_halo(): lax.ppermute(leading, axis, [(b, a) for a, b in up])  16 us
    slice x11, local copies, waits for them, and re-layouts, with_halo(): last = lax.slice_in_dim(array, length - width, length, axis=dim)  15.4 us
  transfers between devices with their start and end apart: 25, of which 14 were waited for; matrix products, arithmetic and copies ran while one was open for 9% of the time, Pallas kernels for 0%

commit v1 on v0

v1 whole, which is shorter than its diff:
```python
import functools

import jax
import jax.numpy as jnp
from jax import lax
from jax.experimental import pallas as pl
from jax.experimental.pallas import tpu as pltpu
from jax.sharding import PartitionSpec as P

STEPS = 4
CHUNKS = 8
MESH = pl.DeviceIdType.MESH
PAD = 8


def leapfrog(dims, f_hbm, e_hbm, c_hbm, out, stat, fld, csq, acc, gath, jsend, jrecv, ksend, krecv, isend, irecv, tsend, trecv, local):
    nj, ni, nk, npy, npx, npz = dims
    rows = ni // CHUNKS
    y, x, z = lax.axis_index("py"), lax.axis_index("px"), lax.axis_index("pz")
    k0, k1 = PAD, PAD + nk
    inner = pl.ds(k0, nk)
    sides = {"py": (y, npy), "px": (x, npx), "pz": (z, npz)}

    def has(axis, side):
        index, count = sides[axis]
        return index > 0 if side == 0 else index < count - 1

    def beside(axis, side):
        return {axis: sides[axis][0] + (2 * side - 1)}

    def load_faces(m, side):
        return pltpu.make_async_copy(
            f_hbm.at[(nj - 1) * side, pl.ds(m * rows, rows)],
            fld.at[0, 1 + (nj - 1) * side, pl.ds(1 + m * rows, rows), inner],
            local.at[side, m],
        )

    def load_inner(m):
        return pltpu.make_async_copy(
            f_hbm.at[pl.ds(1, nj - 2), pl.ds(m * rows, rows)],
            fld.at[0, pl.ds(2, nj - 2), pl.ds(1 + m * rows, rows), inner],
            local.at[2, m],
        )

    def load_earlier(m):
        return pltpu.make_async_copy(
            e_hbm.at[:, pl.ds(m * rows, rows)],
            fld.at[1, pl.ds(1, nj), pl.ds(1 + m * rows, rows), inner],
            local.at[3, m],
        )

    def load_speed(m):
        return pltpu.make_async_copy(c_hbm.at[:, pl.ds(m * rows, rows)], csq.at[:, pl.ds(m * rows, rows)], local.at[4, m])

    def plane(p, m, side):
        span = pl.ds(1 + m * rows, rows)
        return pltpu.make_async_remote_copy(
            fld.at[p, 1 + (nj - 1) * side, span, inner],
            fld.at[p, (nj + 1) * (1 - side), span, inner],
            jsend.at[p, side, m], jrecv.at[p, 1 - side, m],
            device_id=beside("py", side), device_id_type=MESH,
        )

    def edge_k(p, m, side):
        span = pl.ds(1 + m * rows, rows)
        return pltpu.make_async_remote_copy(
            fld.at[p, pl.ds(1, nj), span, pl.ds((k1 - 1) if side else k0, 1)],
            fld.at[p, pl.ds(1, nj), span, pl.ds((k0 - 1) if side else k1, 1)],
            ksend.at[p, side, m], krecv.at[p, 1 - side, m],
            device_id=beside("pz", side), device_id_type=MESH,
        )

    def edge_i(p, side):
        return pltpu.make_async_remote_copy(
            fld.at[p, pl.ds(1, nj), ni if side else 1, inner],
            fld.at[p, pl.ds(1, nj), 0 if side else ni + 1, inner],
            isend.at[p, side], irecv.at[p, 1 - side],
            device_id=beside("px", side), device_id_type=MESH,
        )

    def wait_from(copy):
        copy.wait_recv()

    def each_side(axis, do):
        for side in (0, 1):
            pl.when(has(axis, side))(functools.partial(do, side))

    def over_chunks(do):
        def body(m, _):
            do(m)
            return 0
        lax.fori_loop(0, CHUNKS, body, 0)

    def start_loads(m):
        load_faces(m, 0).start()
        load_faces(m, 1).start()

    over_chunks(start_loads)

    def start_rest(m):
        load_inner(m).start()
        load_earlier(m).start()
        load_speed(m).start()

    over_chunks(start_rest)

    barrier = pltpu.get_barrier_semaphore()
    expected = jnp.int32(npx - 1)
    for axis in ("py", "pz"):
        for side in (0, 1):
            expected = expected + has(axis, side).astype(jnp.int32)

            @pl.when(has(axis, side))
            def _(axis=axis, side=side):
                pl.semaphore_signal(barrier, inc=1, device_id=beside(axis, side), device_id_type=MESH)

    for hop in range(1, npx):
        pl.semaphore_signal(barrier, inc=1, device_id={"px": lax.rem(x + hop, npx)}, device_id_type=MESH)
    pl.semaphore_wait(barrier, expected)

    def first_planes(m):
        load_faces(m, 0).wait()
        load_faces(m, 1).wait()
        each_side("py", lambda side: plane(0, m, side).start())

    over_chunks(first_planes)

    def first_edges(m):
        load_inner(m).wait()
        each_side("pz", lambda side: edge_k(0, m, side).start())

    over_chunks(first_edges)
    each_side("px", lambda side: edge_i(0, side).start())

    for side in (0, 1):
        @pl.when(jnp.logical_not(has("py", side)))
        def _(side=side):
            def clear(i, _):
                for p in (0, 1):
                    fld[p, (nj + 1) * side, i + 1, k0:k1] = jnp.zeros((nk, fld.shape[-1]), jnp.float32)
                return 0
            lax.fori_loop(0, ni, clear, 0)

        @pl.when(jnp.logical_not(has("px", side)))
        def _(side=side):
            for p in (0, 1):
                for j in range(nj):
                    fld[p, j + 1, (ni + 1) * side, k0:k1] = jnp.zeros((nk, fld.shape[-1]), jnp.float32)

        @pl.when(jnp.logical_not(has("pz", side)))
        def _(side=side):
            at = k1 if side else k0 - 8
            def clear(i, _):
                for p in (0, 1):
                    for j in range(nj):
                        fld[p, j + 1, i + 1, at:at + 8] = jnp.zeros((8, fld.shape[-1]), jnp.float32)
                return 0
            lax.fori_loop(0, ni, clear, 0)

    def advance(s, m):
        p, q = s % 2, 1 - s % 2
        last = s == STEPS - 1
        first = m * rows
        for j in range(nj):
            if last:
                shift = fld[p, j + 1, 1, k0:k1]

            def row(r, carry):
                before, middle = carry[:2]
                i = first + r + 1
                after = fld[p, j + 1, i + 1, k0:k1]
                along_j = fld[p, j, i, k0:k1] + fld[p, j + 2, i, k0:k1]
                along_k = fld[p, j + 1, i, k0 - 1:k1 - 1] + fld[p, j + 1, i, k0 + 1:k1 + 1]
                spread = (along_j + (before + after)) + along_k - 6.0 * middle
                later = 2.0 * middle - fld[q, j + 1, i, k0:k1] + csq[j, i - 1] * spread
                if not last:
                    fld[q, j + 1, i, k0:k1] = later
                    return middle, after
                out[j, i - 1] = later
                moved = later - shift
                return middle, after, carry[2] + moved, carry[3] + moved * moved

            carry = (fld[p, j + 1, first, k0:k1], fld[p, j + 1, first + 1, k0:k1])
            if last:
                carry = carry + (acc[0, j], acc[1, j])
            carry = lax.fori_loop(0, rows, row, carry, unroll=4)
            if last:
                acc[0, j] = carry[2]
                acc[1, j] = carry[3]

    acc[...] = jnp.zeros_like(acc)
    for s in range(STEPS):
        p, q = s % 2, 1 - s % 2

        def chunk(m, s=s, p=p, q=q):
            if s == 0:
                load_earlier(m).wait()
                load_speed(m).wait()
            each_side("pz", lambda side: edge_k(p, m, 1 - side).wait_recv())
            for side, at in ((0, 0), (1, CHUNKS - 1)):
                @pl.when(jnp.logical_and(has("px", side), m == at))
                def _(side=side):
                    edge_i(p, 1 - side).wait_recv()
            if s > 0:
                each_side("py", lambda side: plane(q, m, side).wait_send())
                each_side("pz", lambda side: edge_k(q, m, side).wait_send())
                for side, at in ((0, 0), (1, CHUNKS - 1)):
                    @pl.when(jnp.logical_and(has("px", side), m == at))
                    def _(side=side):
                        edge_i(q, side).wait_send()
            each_side("py", lambda side: plane(p, m, 1 - side).wait_recv())
            advance(s, m)
            if s < STEPS - 1:
                each_side("py", lambda side: plane(q, m, side).start())
                each_side("pz", lambda side: edge_k(q, m, side).start())
                for side, at in ((0, 0), (1, CHUNKS - 1)):
                    @pl.when(jnp.logical_and(has("px", side), m == at))
                    def _(side=side):
                        edge_i(q, side).start()

        over_chunks(chunk)

    shift = fld[(STEPS - 1) % 2, 1:1 + nj, 1, k0:k1]
    mean = acc[0] * (1.0 / ni)
    gath[x, 0] = shift + mean
    gath[x, 1] = acc[1] - acc[0] * mean

    def totals(hop):
        return pltpu.make_async_remote_copy(
            gath.at[x], gath.at[x], tsend.at[hop - 1], trecv.at[hop - 1],
            device_id={"px": lax.rem(x + hop, npx)}, device_id_type=MESH,
        )

    for hop in range(1, npx):
        totals(hop).start()
    p = (STEPS - 1) % 2

    def finish(m):
        each_side("py", lambda side: plane(p, m, side).wait_send())
        each_side("pz", lambda side: edge_k(p, m, side).wait_send())

    over_chunks(finish)
    each_side("px", lambda side: edge_i(p, side).wait_send())
    for hop in range(1, npx):
        totals(hop).wait()
    whole = gath[0, 0]
    for n in range(1, npx):
        whole = whole + gath[n, 0]
    whole = whole * (1.0 / npx)
    squares = jnp.zeros_like(whole)
    for n in range(npx):
        off = gath[n, 0] - whole
        squares = squares + (gath[n, 1] + ni * (off * off))
    stat[0] = whole
    stat[1] = lax.rsqrt(squares * (1.0 / (ni * npx)) + 0.0001)


def normalise(f_ref, stat_ref, anomaly_hbm, end_hbm, staged, sems, end_sem):
    nj, ni = f_ref.shape[:2]
    rows = ni // CHUNKS
    ends = [pltpu.make_async_copy(f_ref.at[j], end_hbm.at[j], end_sem.at[j]) for j in range(nj)]
    for copy in ends:
        copy.start()

    def leave(m):
        return pltpu.make_async_copy(
            staged.at[:, pl.ds(m * rows, rows)], anomaly_hbm.at[:, pl.ds(m * rows, rows)], sems.at[m]
        )

    def chunk(m, _):
        for j in range(nj):
            mean, scale = stat_ref[0, j], stat_ref[1, j]

            def row(r, _):
                staged[j, m * rows + r] = (f_ref[j, m * rows + r] - mean) * scale
                return 0

            lax.fori_loop(0, rows, row, 0, unroll=4)
        leave(m).start()
        return 0

    lax.fori_loop(0, CHUNKS, chunk, 0)

    def done(m, _):
        leave(m).wait()
        return 0

    lax.fori_loop(0, CHUNKS, done, 0)
    for copy in ends:
        copy.wait()


def solution(mesh):
    npy, npx, npz = (mesh.shape[a] for a in ("py", "px", "pz"))

    def shards(field_now, earlier, speed_square):
        nj, ni, nk, nl = field_now.shape
        f32 = jnp.float32
        dma = pltpu.SemaphoreType.DMA
        hbm = pl.BlockSpec(memory_space=pltpu.HBM)
        vmem = pl.BlockSpec(memory_space=pltpu.VMEM)
        end, stat = pl.pallas_call(
            functools.partial(leapfrog, (nj, ni, nk, npy, npx, npz)),
            out_shape=(pltpu.VMEM((nj, ni, nk, nl), f32), pltpu.VMEM((2, nj, nk, nl), f32)),
            in_specs=[hbm] * 3,
            out_specs=(vmem, vmem),
            scratch_shapes=[
                pltpu.VMEM((2, nj + 2, ni + 2, nk + 2 * PAD, nl), f32),
                pltpu.VMEM((nj, ni, nk, nl), f32),
                pltpu.VMEM((2, nj, nk, nl), f32),
                pltpu.VMEM((npx, 2, nj, nk, nl), f32),
                dma((2, 2, CHUNKS)), dma((2, 2, CHUNKS)),
                dma((2, 2, CHUNKS)), dma((2, 2, CHUNKS)),
                dma((2, 2)), dma((2, 2)),
                dma((npx - 1,)), dma((npx - 1,)),
                dma((5, CHUNKS)),
            ],
            compiler_params=pltpu.CompilerParams(
                collective_id=0, has_side_effects=True, vmem_limit_bytes=48 << 20
            ),
            name="leapfrog",
        )(field_now, earlier, speed_square)
        return pl.pallas_call(
            normalise,
            out_shape=(jax.ShapeDtypeStruct((nj, ni, nk, nl), f32),) * 2,
            in_specs=[vmem, vmem],
            out_specs=(hbm, hbm),
            scratch_shapes=[pltpu.VMEM((nj, ni, nk, nl), f32), dma((CHUNKS,)), dma((nj,))],
            compiler_params=pltpu.CompilerParams(vmem_limit_bytes=20 << 20),
            name="normalise",
        )(end, stat)

    spec = P("py", "px", "pz", None)
    return jax.shard_map(shards, mesh=mesh, in_specs=(spec,) * 3, out_specs=(spec,) * 2, check_vma=False)
```

time: 384 us -> 203 us (0.53); the launches traced: 379 us -> 203 us
  Pallas kernels: 0 us -> 202 us
  waiting for transfers between devices: 141 us -> 0 us
  other arithmetic: 119 us -> 0 us
  local copies, waits for them, and re-layouts: 59.7 us -> 0 us
  starting transfers between devices: 57.2 us -> 0 us
    pallas_call x0 -> x2, Pallas kernels: none -> 202 us  [the longest x1 197 us: shards(): pl.pallas_call(functools.partial(leapfrog, (nj, ni, nk, npy, npx, npz)),...]
    ppermute x24 -> x0, waiting for transfers between devices: 141 us -> none  [the longest x12 112 us: with_halo(): lax.ppermute(last, axis, up)]
    add x4 -> x0, other arithmetic: 84.8 us -> none  [the longest x3 84.8 us: advance(): return 2.0 * middle - before + speed_square * spread]
    ppermute x24 -> x0, starting transfers between devices: 51.7 us -> none  [the longest x12 35.7 us: with_halo(): lax.ppermute(last, axis, up)]
    unnamed x13 -> x0, local copies, waits for them, and re-layouts: 37.9 us -> none
    reduce_sum x2 -> x0, other arithmetic: 29.5 us -> none  [the longest x1 29 us: shards(): jnp.sum(moved, axis=1, keepdims=True)]
    slice x12 -> x0, local copies, waits for them, and re-layouts: 17.1 us -> none  [the longest x11 15.4 us: with_halo(): last = lax.slice_in_dim(array, length - width, length, axis=dim)]
    all_to_all x1 -> x0, starting transfers between devices: 5.53 us -> none  [copy_for_each(): lax.all_to_all(jnp.broadcast_to(array[None], (devices, *array.shape)), ax...]
  transfers between devices with their start and end apart: 25 -> 0, of which waited for: 14 -> 0; matrix products, arithmetic and copies ran while one was open for 9% -> 0% of each run, Pallas kernels for 0% -> 0%
where the time goes in v1:
time: 203 us
  Pallas kernels  202 us (100%)
    pallas_call x1, Pallas kernels, shards(): pl.pallas_call(functools.partial(leapfrog, (nj, ni, nk, npy, npx, npz)),...  197 us
    pallas_call x1, Pallas kernels, shards(): pl.pallas_call(normalise, out_shape=(jax.ShapeDtypeStruct((nj, ni, nk, nl...  5.93 us

profile of v1, /device:TPU:0, one launch (start us, length us, event | category | flops | bytes accessed | tf_op | source)
XLA Modules:
  0.0 203.1 jit_solution(10665613921361141507)
XLA Ops:
  0.6 196.6 %leapfrog.1 = (f32[4,128,32,128]{3,2,1,0:T(8,128)S(1)}, f32[2,4,32,128]{3,2,1,0:T(8,128)S(1)}) custom-call(f32[4,128,32,128]{3,2,1,0:T(8,128)} %f_hbm.1, f32[4,128,32,128]{3,2,1,0:T(8,128)} %e_hbm.1, f32[4,128,32,128]{3,2,1,0:T(8,128)} %c_hbm.1), custom_call_target="tpu_custom_call" | custom-call | tf_op jit(solution)/shard_map/leapfrog/pallas_call | solution.py:302
  197.2 5.9 %normalise.1 = (f32[4,128,32,128]{3,2,1,0:T(8,128)}, f32[4,128,32,128]{3,2,1,0:T(8,128)}) custom-call(f32[4,128,32,128]{3,2,1,0:T(8,128)S(1)} %get-tuple-element.4.f_ref, f32[2,4,32,128]{3,2,1,0:T(8,128)S(1)} %get-tuple-element.5.stat_ref), custom_call_target="tpu_custom_call" | custom-call | tf_op jit(solution)/shard_map/normalise/pallas_call | solution.py:323

commit v2 on v1

--- a/solution.py
+++ b/solution.py
@@ -9,13 +9,17 @@
 
 STEPS = 4
 CHUNKS = 8
+SPANS = 4
+TILE = 8
 MESH = pl.DeviceIdType.MESH
 PAD = 8
 
 
-def leapfrog(dims, f_hbm, e_hbm, c_hbm, out, stat, fld, csq, acc, gath, jsend, jrecv, ksend, krecv, isend, irecv, tsend, trecv, local):
+def leapfrog(dims, f_hbm, e_hbm, c_hbm, out, stat, fld, csq, acc, inner_sums, face_sums, jsend, jrecv, lsend, lrecv, ksend, krecv, isend, irecv, tsend, trecv, local):
     nj, ni, nk, npy, npx, npz = dims
-    rows = ni // CHUNKS
+    rows, long = ni // CHUNKS, ni // SPANS
+    tiles = nk // TILE
+    final = (STEPS - 1) % 2
     y, x, z = lax.axis_index("py"), lax.axis_index("px"), lax.axis_index("pz")
     k0, k1 = PAD, PAD + nk
     inner = pl.ds(k0, nk)
@@ -58,6 +62,15 @@
             fld.at[p, 1 + (nj - 1) * side, span, inner],
             fld.at[p, (nj + 1) * (1 - side), span, inner],
             jsend.at[p, side, m], jrecv.at[p, 1 - side, m],
+            device_id=beside("py", side), device_id_type=MESH,
+        )
+
+    def last_plane(q, h, side):
+        span, tile = pl.ds(1 + h * long, long), pl.ds(k0 + q * TILE, TILE)
+        return pltpu.make_async_remote_copy(
+            fld.at[final, 1 + (nj - 1) * side, span, tile],
+            fld.at[final, (nj + 1) * (1 - side), span, tile],
+            lsend.at[side, q, h], lrecv.at[1 - side, q, h],
             device_id=beside("py", side), device_id_type=MESH,
         )
 
@@ -157,39 +170,31 @@
                 return 0
             lax.fori_loop(0, ni, clear, 0)
 
-    def advance(s, m):
-        p, q = s % 2, 1 - s % 2
-        last = s == STEPS - 1
-        first = m * rows
-        for j in range(nj):
-            if last:
-                shift = fld[p, j + 1, 1, k0:k1]
-
-            def row(r, carry):
-                before, middle = carry[:2]
-                i = first + r + 1
-                after = fld[p, j + 1, i + 1, k0:k1]
-                along_j = fld[p, j, i, k0:k1] + fld[p, j + 2, i, k0:k1]
-                along_k = fld[p, j + 1, i, k0 - 1:k1 - 1] + fld[p, j + 1, i, k0 + 1:k1 + 1]
-                spread = (along_j + (before + after)) + along_k - 6.0 * middle
-                later = 2.0 * middle - fld[q, j + 1, i, k0:k1] + csq[j, i - 1] * spread
-                if not last:
-                    fld[q, j + 1, i, k0:k1] = later
-                    return middle, after
-                out[j, i - 1] = later
-                moved = later - shift
-                return middle, after, carry[2] + moved, carry[3] + moved * moved
-
-            carry = (fld[p, j + 1, first, k0:k1], fld[p, j + 1, first + 1, k0:k1])
-            if last:
-                carry = carry + (acc[0, j], acc[1, j])
-            carry = lax.fori_loop(0, rows, row, carry, unroll=4)
-            if last:
-                acc[0, j] = carry[2]
-                acc[1, j] = carry[3]
-
-    acc[...] = jnp.zeros_like(acc)
-    for s in range(STEPS):
+    def advance(p, j, first, count, ks, put, shift=None, sums=None):
+        lo, hi = k0 + ks[0], k0 + ks[1]
+
+        def row(r, carry):
+            before, middle = carry[:2]
+            i = first + r + 1
+            after = fld[p, j + 1, i + 1, lo:hi]
+            along_j = fld[p, j, i, lo:hi] + fld[p, j + 2, i, lo:hi]
+            along_k = fld[p, j + 1, i, lo - 1:hi - 1] + fld[p, j + 1, i, lo + 1:hi + 1]
+            spread = (along_j + (before + after)) + along_k - 6.0 * middle
+            later = 2.0 * middle - fld[1 - p, j + 1, i, lo:hi] + csq[j, i - 1, ks[0]:ks[1]] * spread
+            put(i - 1, later)
+            if sums is None:
+                return middle, after
+            moved = later - shift
+            return middle, after, carry[2] + moved, carry[3] + moved * moved
+
+        carry = (fld[p, j + 1, first, lo:hi], fld[p, j + 1, first + 1, lo:hi]) + (sums or ())
+        return lax.fori_loop(0, count, row, carry, unroll=4)[2:]
+
+    def with_edges(m, do):
+        for side, at in ((0, 0), (1, CHUNKS - 1)):
+            pl.when(jnp.logical_and(has("px", side), m == at))(functools.partial(do, side))
+
+    for s in range(STEPS - 1):
         p, q = s % 2, 1 - s % 2
 
         def chunk(m, s=s, p=p, q=q):
@@ -197,62 +202,129 @@
                 load_earlier(m).wait()
                 load_speed(m).wait()
             each_side("pz", lambda side: edge_k(p, m, 1 - side).wait_recv())
-            for side, at in ((0, 0), (1, CHUNKS - 1)):
-                @pl.when(jnp.logical_and(has("px", side), m == at))
-                def _(side=side):
-                    edge_i(p, 1 - side).wait_recv()
+            with_edges(m, lambda side: edge_i(p, 1 - side).wait_recv())
             if s > 0:
                 each_side("py", lambda side: plane(q, m, side).wait_send())
                 each_side("pz", lambda side: edge_k(q, m, side).wait_send())
-                for side, at in ((0, 0), (1, CHUNKS - 1)):
-                    @pl.when(jnp.logical_and(has("px", side), m == at))
-                    def _(side=side):
-                        edge_i(q, side).wait_send()
+                with_edges(m, lambda side: edge_i(q, side).wait_send())
             each_side("py", lambda side: plane(p, m, 1 - side).wait_recv())
-            advance(s, m)
-            if s < STEPS - 1:
+            for j in range(nj):
+                def put(i, later, j=j):
+                    fld[q, j + 1, i + 1, k0:k1] = later
+
+                advance(p, j, m * rows, rows, (0, nk), put)
+            if s < STEPS - 2:
                 each_side("py", lambda side: plane(q, m, side).start())
-                each_side("pz", lambda side: edge_k(q, m, side).start())
-                for side, at in ((0, 0), (1, CHUNKS - 1)):
-                    @pl.when(jnp.logical_and(has("px", side), m == at))
-                    def _(side=side):
-                        edge_i(q, side).start()
+            else:
+                per = CHUNKS // SPANS
+
+                @pl.when(lax.rem(m, per) == per - 1)
+                def _():
+                    each_side("py", lambda side: last_plane(0, m // per, side).start())
+            each_side("pz", lambda side: edge_k(q, m, side).start())
+            with_edges(m, lambda side: edge_i(q, side).start())
 
         over_chunks(chunk)
 
-    shift = fld[(STEPS - 1) % 2, 1:1 + nj, 1, k0:k1]
-    mean = acc[0] * (1.0 / ni)
-    gath[x, 0] = shift + mean
-    gath[x, 1] = acc[1] - acc[0] * mean
-
-    def totals(hop):
-        return pltpu.make_async_remote_copy(
-            gath.at[x], gath.at[x], tsend.at[hop - 1], trecv.at[hop - 1],
-            device_id={"px": lax.rem(x + hop, npx)}, device_id_type=MESH,
-        )
-
-    for hop in range(1, npx):
-        totals(hop).start()
-    p = (STEPS - 1) % 2
+    def over_spans(do):
+        def body(h, _):
+            do(h)
+            return 0
+        lax.fori_loop(0, SPANS, body, 0)
+
+    for q in range(1, tiles):
+        over_spans(lambda h, q=q: each_side("py", lambda side: last_plane(q, h, side).start()))
+
+    p = final
+    peers = [lax.rem(x + hop, npx) for hop in range(1, npx)]
+
+    def share(buffer, group):
+        return [
+            pltpu.make_async_remote_copy(
+                buffer.at[x], buffer.at[x], tsend.at[group, n], trecv.at[group, n],
+                device_id={"px": peer}, device_id_type=MESH,
+            )
+            for n, peer in enumerate(peers)
+        ]
+
+    def local_sums(first, second, shift):
+        mean = first * (1.0 / ni)
+        return shift + mean, second - first * mean
+
+    def line_sums(parts):
+        mean = parts[0][0]
+        for part in parts[1:]:
+            mean = mean + part[0]
+        mean = mean * (1.0 / npx)
+        squares = jnp.zeros_like(mean)
+        for part in parts:
+            off = part[0] - mean
+            squares = squares + (part[1] + ni * (off * off))
+        return mean, lax.rsqrt(squares * (1.0 / (ni * npx)) + 0.0001)
+
+    over_chunks(lambda m: each_side("pz", lambda side: edge_k(p, m, 1 - side).wait_recv()))
+    each_side("px", lambda side: edge_i(p, 1 - side).wait_recv())
+    for j in range(1, nj - 1):
+        def put(i, later, j=j):
+            out[j, i] = later
+
+        shift = fld[p, j + 1, 1, k0:k1]
+        zero = jnp.zeros_like(shift)
+        sums = advance(p, j, 0, ni, (0, nk), put, shift, (zero, zero))
+        inner_sums[x, 0, j - 1], inner_sums[x, 1, j - 1] = local_sums(*sums, shift)
+    for copy in share(inner_sums, tiles):
+        copy.start()
+
+    def settle_inner():
+        for copy in share(inner_sums, tiles):
+            copy.wait()
+        mean, scale = line_sums([(inner_sums[n, 0], inner_sums[n, 1]) for n in range(npx)])
+        stat[0, 1:nj - 1] = mean
+        stat[1, 1:nj - 1] = scale
+
+    def settle_faces(q):
+        for copy in share(face_sums.at[q], q):
+            copy.wait()
+        for f, j in enumerate((0, nj - 1)):
+            mean, scale = line_sums([(face_sums[q, n, 0, f], face_sums[q, n, 1, f]) for n in range(npx)])
+            stat[0, j, q * TILE:(q + 1) * TILE] = mean
+            stat[1, j, q * TILE:(q + 1) * TILE] = scale
+
+    for q in range(tiles):
+        ks = (q * TILE, (q + 1) * TILE)
+        shifts = [fld[p, j + 1, 1, k0 + ks[0]:k0 + ks[1]] for j in (0, nj - 1)]
+        acc[...] = jnp.zeros_like(acc)
+
+        def span(h, q=q, ks=ks, shifts=shifts):
+            each_side("py", lambda side: last_plane(q, h, 1 - side).wait_recv())
+            for f, j in enumerate((0, nj - 1)):
+                def put(i, later, j=j):
+                    out[j, i, ks[0]:ks[1]] = later
+
+                acc[f, 0], acc[f, 1] = advance(p, j, h * long, long, ks, put, shifts[f], (acc[f, 0], acc[f, 1]))
+
+        over_spans(span)
+        for f in range(2):
+            face_sums[q, x, 0, f], face_sums[q, x, 1, f] = local_sums(acc[f, 0], acc[f, 1], shifts[f])
+        for copy in share(face_sums.at[q], q):
+            copy.start()
+        if q == 0:
+            settle_inner()
+        else:
+            settle_faces(q - 1)
+
+    for q in range(tiles):
+        over_spans(lambda h, q=q: each_side("py", lambda side: last_plane(q, h, side).wait_send()))
 
     def finish(m):
-        each_side("py", lambda side: plane(p, m, side).wait_send())
+        each_side("py", lambda side: plane(1 - p, m, side).wait_send())
+        each_side("pz", lambda side: edge_k(1 - p, m, side).wait_send())
         each_side("pz", lambda side: edge_k(p, m, side).wait_send())
 
     over_chunks(finish)
-    each_side("px", lambda side: edge_i(p, side).wait_send())
-    for hop in range(1, npx):
-        totals(hop).wait()
-    whole = gath[0, 0]
-    for n in range(1, npx):
-        whole = whole + gath[n, 0]
-    whole = whole * (1.0 / npx)
-    squares = jnp.zeros_like(whole)
-    for n in range(npx):
-        off = gath[n, 0] - whole
-        squares = squares + (gath[n, 1] + ni * (off * off))
-    stat[0] = whole
-    stat[1] = lax.rsqrt(squares * (1.0 / (ni * npx)) + 0.0001)
+    for t in (1 - p, p):
+        each_side("px", lambda side: edge_i(t, side).wait_send())
+    settle_faces(tiles - 1)
 
 
 def normalise(f_ref, stat_ref, anomaly_hbm, end_hbm, staged, sems, end_sem):
@@ -307,12 +379,14 @@
             scratch_shapes=[
                 pltpu.VMEM((2, nj + 2, ni + 2, nk + 2 * PAD, nl), f32),
                 pltpu.VMEM((nj, ni, nk, nl), f32),
-                pltpu.VMEM((2, nj, nk, nl), f32),
-                pltpu.VMEM((npx, 2, nj, nk, nl), f32),
+                pltpu.VMEM((2, 2, TILE, nl), f32),
+                pltpu.VMEM((npx, 2, nj - 2, nk, nl), f32),
+                pltpu.VMEM((nk // TILE, npx, 2, 2, TILE, nl), f32),
                 dma((2, 2, CHUNKS)), dma((2, 2, CHUNKS)),
+                dma((2, nk // TILE, SPANS)), dma((2, nk // TILE, SPANS)),
                 dma((2, 2, CHUNKS)), dma((2, 2, CHUNKS)),
                 dma((2, 2)), dma((2, 2)),
-                dma((npx - 1,)), dma((npx - 1,)),
+                dma((nk // TILE + 1, npx - 1)), dma((nk // TILE + 1, npx - 1)),
                 dma((5, CHUNKS)),
             ],
             compiler_params=pltpu.CompilerParams(

time: 203 us -> 200 us (0.985)
  Pallas kernels: 202 us -> 199 us
    pallas_call x1, Pallas kernels: 197 us -> 193 us  [shards(): pl.pallas_call(functools.partial(leapfrog, (nj, ni, nk, npy, npx, npz)),...]
where the time goes in v2:
time: 200 us; the launch traced here: 199 us
  Pallas kernels  199 us (100%)
    pallas_call x1, Pallas kernels, shards(): pl.pallas_call(functools.partial(leapfrog, (nj, ni, nk, npy, npx, npz)),...  193 us
    pallas_call x1, Pallas kernels, shards(): pl.pallas_call(normalise, out_shape=(jax.ShapeDtypeStruct((nj, ni, nk, nl...  5.93 us

profile of v2, /device:TPU:0, one launch (start us, length us, event | category | flops | bytes accessed | tf_op | source)
XLA Modules:
  0.0 199.5 jit_solution(3954989065420988857)
XLA Ops:
  0.6 192.9 %leapfrog.1 = (f32[4,128,32,128]{3,2,1,0:T(8,128)S(1)}, f32[2,4,32,128]{3,2,1,0:T(8,128)S(1)}) custom-call(f32[4,128,32,128]{3,2,1,0:T(8,128)} %f_hbm.1, f32[4,128,32,128]{3,2,1,0:T(8,128)} %e_hbm.1, f32[4,128,32,128]{3,2,1,0:T(8,128)} %c_hbm.1), custom_call_target="tpu_custom_call" | custom-call | tf_op jit(solution)/shard_map/leapfrog/pallas_call | solution.py:374
  193.5 5.9 %normalise.1 = (f32[4,128,32,128]{3,2,1,0:T(8,128)}, f32[4,128,32,128]{3,2,1,0:T(8,128)}) custom-call(f32[4,128,32,128]{3,2,1,0:T(8,128)S(1)} %get-tuple-element.4.f_ref, f32[2,4,32,128]{3,2,1,0:T(8,128)S(1)} %get-tuple-element.5.stat_ref), custom_call_target="tpu_custom_call" | custom-call | tf_op jit(solution)/shard_map/normalise/pallas_call | solution.py:397

commit v3 on v2

v3 whole, which is shorter than its diff:
```python
import functools

import jax
import jax.numpy as jnp
from jax import lax
from jax.experimental import pallas as pl
from jax.experimental.pallas import tpu as pltpu
from jax.sharding import PartitionSpec as P

STEPS = 4
CHUNKS = 4
SPANS = 4
TILE = 8
PARTS = 8
MESH = pl.DeviceIdType.MESH
PAD = 8


def leapfrog(dims, f_hbm, e_hbm, c_hbm, out, stat, fld, csq, acc, inner_sums, face_sums, jsend, jrecv, lsend, lrecv, ksend, krecv, isend, irecv, tsend, trecv, local):
    nj, ni, nk, npy, npx, npz = dims
    rows, long = ni // CHUNKS, ni // SPANS
    tiles = nk // TILE
    final = (STEPS - 1) % 2
    y, x, z = lax.axis_index("py"), lax.axis_index("px"), lax.axis_index("pz")
    k0, k1 = PAD, PAD + nk
    inner = pl.ds(k0, nk)
    everything = pl.ds(1, ni)
    sides = {"py": (y, npy), "px": (x, npx), "pz": (z, npz)}

    def has(axis, side):
        index, count = sides[axis]
        return index > 0 if side == 0 else index < count - 1

    def beside(axis, side):
        return {axis: sides[axis][0] + (2 * side - 1)}

    def span_of(m):
        return pl.ds(1 + m * rows, rows)

    def load_faces(side, part):
        start, size = ((0, rows), (rows, ni - rows))[part]
        return pltpu.make_async_copy(
            f_hbm.at[(nj - 1) * side, pl.ds(start, size)],
            fld.at[0, 1 + (nj - 1) * side, pl.ds(1 + start, size), inner],
            local.at[2 * part + side],
        )

    def load_inner():
        return pltpu.make_async_copy(
            f_hbm.at[pl.ds(1, nj - 2)], fld.at[0, pl.ds(2, nj - 2), everything, inner], local.at[4]
        )

    def load_earlier():
        return pltpu.make_async_copy(e_hbm, fld.at[1, pl.ds(1, nj), everything, inner], local.at[5])

    def load_speed():
        return pltpu.make_async_copy(c_hbm, csq, local.at[6])

    def face_copy(p, span, tile, side, sent, received):
        return pltpu.make_async_remote_copy(
            fld.at[p, 1 + (nj - 1) * side, span, tile],
            fld.at[p, (nj + 1) * (1 - side), span, tile],
            sent, received, device_id=beside("py", side), device_id_type=MESH,
        )

    def plane(p, m, side):
        return face_copy(p, span_of(m), inner, side, jsend.at[p, side], jrecv.at[p, 1 - side, m])

    def sent_planes(p, side):
        return face_copy(p, everything, inner, side, jsend.at[p, side], jrecv.at[p, 1 - side, 0])

    def last_plane(q, h, side):
        span = everything if h is None else pl.ds(1 + h * long, long)
        slot = tiles - 1 + h if q == tiles - 1 else q
        return face_copy(final, span, pl.ds(k0 + q * TILE, TILE), side, lsend.at[side], lrecv.at[1 - side, slot])

    def sent_last(side):
        return face_copy(final, everything, inner, side, lsend.at[side], lrecv.at[1 - side, 0])

    def edge_k(p, m, side):
        span = everything if m is None else span_of(m)
        return pltpu.make_async_remote_copy(
            fld.at[p, pl.ds(1, nj), span, pl.ds((k1 - 1) if side else k0, 1)],
            fld.at[p, pl.ds(1, nj), span, pl.ds((k0 - 1) if side else k1, 1)],
            ksend.at[p, side], krecv.at[p, 1 - side],
            device_id=beside("pz", side), device_id_type=MESH,
        )

    def edge_i(p, side):
        return pltpu.make_async_remote_copy(
            fld.at[p, pl.ds(1, nj), ni if side else 1, inner],
            fld.at[p, pl.ds(1, nj), 0 if side else ni + 1, inner],
            isend.at[p, side], irecv.at[p, 1 - side],
            device_id=beside("px", side), device_id_type=MESH,
        )

    def each_side(axis, do):
        for side in (0, 1):
            pl.when(has(axis, side))(functools.partial(do, side))

    def repeat(count, do, start=0):
        def body(m, _):
            do(m)
            return 0
        lax.fori_loop(start, count, body, 0)

    for part in (0, 1):
        for side in (0, 1):
            load_faces(side, part).start()

    barrier = pltpu.get_barrier_semaphore()
    expected = jnp.int32(0)
    for axis in ("py", "px", "pz"):
        for side in (0, 1):
            expected = expected + has(axis, side).astype(jnp.int32)

            @pl.when(has(axis, side))
            def _(axis=axis, side=side):
                pl.semaphore_signal(barrier, inc=1, device_id=beside(axis, side), device_id_type=MESH)

    pl.semaphore_wait(barrier, expected)

    for part, (start, stop) in enumerate(((0, 1), (1, CHUNKS))):
        for side in (0, 1):
            load_faces(side, part).wait()
        repeat(stop, lambda m: each_side("py", lambda side: plane(0, m, side).start()), start)

    load_inner().start()
    load_earlier().start()
    load_speed().start()
    load_inner().wait()
    each_side("pz", lambda side: edge_k(0, None, side).start())
    each_side("px", lambda side: edge_i(0, side).start())

    for side in (0, 1):
        @pl.when(jnp.logical_not(has("py", side)))
        def _(side=side):
            def clear(i):
                for p in (0, 1):
                    fld[p, (nj + 1) * side, i + 1, k0:k1] = jnp.zeros((nk, fld.shape[-1]), jnp.float32)
            repeat(ni, clear)

        @pl.when(jnp.logical_not(has("px", side)))
        def _(side=side):
            for p in (0, 1):
                for j in range(nj):
                    fld[p, j + 1, (ni + 1) * side, k0:k1] = jnp.zeros((nk, fld.shape[-1]), jnp.float32)

        @pl.when(jnp.logical_not(has("pz", side)))
        def _(side=side):
            at = k1 if side else k0 - 8
            def clear(i):
                for p in (0, 1):
                    for j in range(nj):
                        fld[p, j + 1, i + 1, at:at + 8] = jnp.zeros((8, fld.shape[-1]), jnp.float32)
            repeat(ni, clear)

    def advance(p, j, first, count, ks, put, shift=None, sums=None):
        lo, hi = k0 + ks[0], k0 + ks[1]

        def row(r, carry):
            before, middle = carry[:2]
            i = first + r + 1
            after = fld[p, j + 1, i + 1, lo:hi]
            along_j = fld[p, j, i, lo:hi] + fld[p, j + 2, i, lo:hi]
            along_k = fld[p, j + 1, i, lo - 1:hi - 1] + fld[p, j + 1, i, lo + 1:hi + 1]
            spread = (along_j + (before + after)) + along_k - 6.0 * middle
            later = 2.0 * middle - fld[1 - p, j + 1, i, lo:hi] + csq[j, i - 1, ks[0]:ks[1]] * spread
            put(i - 1, later)
            if sums is None:
                return middle, after
            moved = later - shift
            return middle, after, carry[2] + moved, carry[3] + moved * moved

        carry = (fld[p, j + 1, first, lo:hi], fld[p, j + 1, first + 1, lo:hi]) + (sums or ())
        return lax.fori_loop(0, count, row, carry, unroll=4)[2:]

    def with_edges(m, do):
        for side, at in ((0, 0), (1, CHUNKS - 1)):
            pl.when(jnp.logical_and(has("px", side), m == at))(functools.partial(do, side))

    for s in range(STEPS - 1):
        p, q = s % 2, 1 - s % 2
        if s == 0:
            load_earlier().wait()
            load_speed().wait()
        else:
            each_side("py", lambda side: sent_planes(q, side).wait_send())
            each_side("pz", lambda side: edge_k(q, None, side).wait_send())
            each_side("px", lambda side: edge_i(q, side).wait_send())
        each_side("pz", lambda side: edge_k(p, None, 1 - side).wait_recv())
        each_side("px", lambda side: edge_i(p, 1 - side).wait_recv())

        def chunk(m, s=s, p=p, q=q):
            each_side("py", lambda side: plane(p, m, 1 - side).wait_recv())
            for j in range(nj):
                def put(i, later, j=j):
                    fld[q, j + 1, i + 1, k0:k1] = later

                advance(p, j, m * rows, rows, (0, nk), put)
            if s < STEPS - 2:
                each_side("py", lambda side: plane(q, m, side).start())
            else:
                per = CHUNKS // SPANS

                @pl.when(lax.rem(m, per) == per - 1)
                def _():
                    each_side("py", lambda side: last_plane(0, m // per, side).start())
            each_side("pz", lambda side: edge_k(q, m, side).start())
            with_edges(m, lambda side: edge_i(q, side).start())

        repeat(CHUNKS, chunk)

    for q in range(1, tiles - 1):
        each_side("py", lambda side: last_plane(q, None, side).start())
    repeat(SPANS, lambda h: each_side("py", lambda side: last_plane(tiles - 1, h, side).start()))

    p = final
    peers = [lax.rem(x + hop, npx) for hop in range(1, npx)]

    def share(buffer, group):
        for peer in peers:
            pltpu.make_async_remote_copy(
                buffer.at[x], buffer.at[x], tsend.at[group // tiles], trecv.at[group],
                device_id={"px": peer}, device_id_type=MESH,
            ).start()

    def shared(cells, group):
        return pltpu.make_async_remote_copy(
            cells, cells, tsend.at[group // tiles], trecv.at[group], device_id={"px": peers[0]}, device_id_type=MESH
        )

    others = pl.ds(0, npx - 1)

    def local_sums(first, second, shift):
        mean = first * (1.0 / ni)
        return shift + mean, second - first * mean

    def line_sums(parts):
        mean = parts[0][0]
        for part in parts[1:]:
            mean = mean + part[0]
        mean = mean * (1.0 / npx)
        squares = jnp.zeros_like(mean)
        for part in parts:
            off = part[0] - mean
            squares = squares + (part[1] + ni * (off * off))
        return mean, lax.rsqrt(squares * (1.0 / (ni * npx)) + 0.0001)

    each_side("pz", lambda side: edge_k(p, None, 1 - side).wait_recv())
    each_side("px", lambda side: edge_i(p, 1 - side).wait_recv())
    for j in range(1, nj - 1):
        def put(i, later, j=j):
            out[j, i] = later

        shift = fld[p, j + 1, 1, k0:k1]
        zero = jnp.zeros_like(shift)
        sums = advance(p, j, 0, ni, (0, nk), put, shift, (zero, zero))
        inner_sums[x, 0, j - 1], inner_sums[x, 1, j - 1] = local_sums(*sums, shift)
    share(inner_sums, tiles)

    def settle_inner():
        shared(inner_sums.at[others], tiles).wait_recv()
        mean, scale = line_sums([(inner_sums[n, 0], inner_sums[n, 1]) for n in range(npx)])
        stat[0, 1:nj - 1] = mean
        stat[1, 1:nj - 1] = scale

    def settle_faces(q):
        shared(face_sums.at[q, others], q).wait_recv()
        for f, j in enumerate((0, nj - 1)):
            mean, scale = line_sums([(face_sums[q, n, 0, f], face_sums[q, n, 1, f]) for n in range(npx)])
            stat[0, j, q * TILE:(q + 1) * TILE] = mean
            stat[1, j, q * TILE:(q + 1) * TILE] = scale

    for q in range(tiles):
        ks = (q * TILE, (q + 1) * TILE)
        shifts = [fld[p, j + 1, 1, k0 + ks[0]:k0 + ks[1]] for j in (0, nj - 1)]
        acc[...] = jnp.zeros_like(acc)

        pieces = SPANS if q == tiles - 1 else 1
        count = ni // pieces

        def span(h, q=q, ks=ks, shifts=shifts, pieces=pieces, count=count):
            each_side("py", lambda side: last_plane(q, h if pieces > 1 else None, 1 - side).wait_recv())
            for f, j in enumerate((0, nj - 1)):
                def put(i, later, j=j):
                    out[j, i, ks[0]:ks[1]] = later

                acc[f, 0], acc[f, 1] = advance(p, j, h * count, count, ks, put, shifts[f], (acc[f, 0], acc[f, 1]))

        repeat(pieces, span)
        for f in range(2):
            face_sums[q, x, 0, f], face_sums[q, x, 1, f] = local_sums(acc[f, 0], acc[f, 1], shifts[f])
        share(face_sums.at[q], q)
        if q == 0:
            settle_inner()
        else:
            settle_faces(q - 1)

    each_side("py", lambda side: sent_last(side).wait_send())
    each_side("py", lambda side: sent_planes(1 - p, side).wait_send())
    for t in (1 - p, p):
        each_side("pz", lambda side: edge_k(t, None, side).wait_send())
        each_side("px", lambda side: edge_i(t, side).wait_send())
    shared(inner_sums.at[others], tiles).wait_send()
    settle_faces(tiles - 1)
    shared(face_sums.at[:, others], 0).wait_send()


def normalise(f_ref, stat_ref, anomaly_hbm, end_hbm, staged, sems):
    nj, ni = f_ref.shape[:2]
    rows = ni // PARTS
    end = pltpu.make_async_copy(f_ref, end_hbm, sems.at[0])
    end.start()

    def chunk(m, _):
        for j in range(nj):
            mean, scale = stat_ref[0, j], stat_ref[1, j]

            def row(r, _):
                staged[j, m * rows + r] = (f_ref[j, m * rows + r] - mean) * scale
                return 0

            lax.fori_loop(0, rows, row, 0, unroll=4)
        piece = pl.ds(m * rows, rows)
        pltpu.make_async_copy(staged.at[:, piece], anomaly_hbm.at[:, piece], sems.at[1]).start()
        return 0

    lax.fori_loop(0, PARTS, chunk, 0)
    end.wait()
    pltpu.make_async_copy(staged, anomaly_hbm, sems.at[1]).wait()


def solution(mesh):
    npy, npx, npz = (mesh.shape[a] for a in ("py", "px", "pz"))

    def shards(field_now, earlier, speed_square):
        nj, ni, nk, nl = field_now.shape
        f32 = jnp.float32
        dma = pltpu.SemaphoreType.DMA
        hbm = pl.BlockSpec(memory_space=pltpu.HBM)
        vmem = pl.BlockSpec(memory_space=pltpu.VMEM)
        end, stat = pl.pallas_call(
            functools.partial(leapfrog, (nj, ni, nk, npy, npx, npz)),
            out_shape=(pltpu.VMEM((nj, ni, nk, nl), f32), pltpu.VMEM((2, nj, nk, nl), f32)),
            in_specs=[hbm] * 3,
            out_specs=(vmem, vmem),
            scratch_shapes=[
                pltpu.VMEM((2, nj + 2, ni + 2, nk + 2 * PAD, nl), f32),
                pltpu.VMEM((nj, ni, nk, nl), f32),
                pltpu.VMEM((2, 2, TILE, nl), f32),
                pltpu.VMEM((npx, 2, nj - 2, nk, nl), f32),
                pltpu.VMEM((nk // TILE, npx, 2, 2, TILE, nl), f32),
                dma((2, 2)), dma((2, 2, CHUNKS)),
                dma((2,)), dma((2, nk // TILE - 1 + SPANS)),
                dma((2, 2)), dma((2, 2)),
                dma((2, 2)), dma((2, 2)),
                dma((2,)), dma((nk // TILE + 1,)),
                dma((7,)),
            ],
            compiler_params=pltpu.CompilerParams(
                collective_id=0, has_side_effects=True, vmem_limit_bytes=48 << 20
            ),
            name="leapfrog",
        )(field_now, earlier, speed_square)
        return pl.pallas_call(
            normalise,
            out_shape=(jax.ShapeDtypeStruct((nj, ni, nk, nl), f32),) * 2,
            in_specs=[vmem, vmem],
            out_specs=(hbm, hbm),
            scratch_shapes=[pltpu.VMEM((nj, ni, nk, nl), f32), dma((2,))],
            compiler_params=pltpu.CompilerParams(vmem_limit_bytes=20 << 20),
            name="normalise",
        )(end, stat)

    spec = P("py", "px", "pz", None)
    return jax.shard_map(shards, mesh=mesh, in_specs=(spec,) * 3, out_specs=(spec,) * 2, check_vma=False)
```

time: 200 us -> 198 us (0.990)
  Pallas kernels: 199 us -> 197 us
    pallas_call x1, Pallas kernels: 193 us -> 191 us  [shards(): pl.pallas_call(functools.partial(leapfrog, (nj, ni, nk, npy, npx, npz)),...]
where the time goes in v3:
time: 198 us; the launch traced here: 197 us
  Pallas kernels  197 us (99%)
    pallas_call x1, Pallas kernels, shards(): pl.pallas_call(functools.partial(leapfrog, (nj, ni, nk, npy, npx, npz)),...  191 us
    pallas_call x1, Pallas kernels, shards(): pl.pallas_call(normalise, out_shape=(jax.ShapeDtypeStruct((nj, ni, nk, nl...  5.96 us

profile of v3, /device:TPU:0, one launch (start us, length us, event | category | flops | bytes accessed | tf_op | source)
XLA Modules:
  0.0 197.5 jit_solution(4325772954997473587)
XLA Ops:
  0.6 190.9 %leapfrog.1 = (f32[4,128,32,128]{3,2,1,0:T(8,128)S(1)}, f32[2,4,32,128]{3,2,1,0:T(8,128)S(1)}) custom-call(f32[4,128,32,128]{3,2,1,0:T(8,128)} %f_hbm.1, f32[4,128,32,128]{3,2,1,0:T(8,128)} %e_hbm.1, f32[4,128,32,128]{3,2,1,0:T(8,128)} %c_hbm.1), custom_call_target="tpu_custom_call" | custom-call | tf_op jit(solution)/shard_map/leapfrog/pallas_call | solution.py:343
  191.5 6.0 %normalise.1 = (f32[4,128,32,128]{3,2,1,0:T(8,128)}, f32[4,128,32,128]{3,2,1,0:T(8,128)}) custom-call(f32[4,128,32,128]{3,2,1,0:T(8,128)S(1)} %get-tuple-element.4.f_ref, f32[2,4,32,128]{3,2,1,0:T(8,128)S(1)} %get-tuple-element.5.stat_ref), custom_call_target="tpu_custom_call" | custom-call | tf_op jit(solution)/shard_map/normalise/pallas_call | solution.py:366

commit v4 on v3

--- a/solution.py
+++ b/solution.py
@@ -155,6 +155,17 @@
                         fld[p, j + 1, i + 1, at:at + 8] = jnp.zeros((8, fld.shape[-1]), jnp.float32)
             repeat(ni, clear)
 
+    def later_at(p, j, i, before, middle, after, ks):
+        lo, hi = k0 + ks[0], k0 + ks[1]
+        along_j = fld[p, j, i, lo:hi] + fld[p, j + 2, i, lo:hi]
+        along_k = fld[p, j + 1, i, lo - 1:hi - 1] + fld[p, j + 1, i, lo + 1:hi + 1]
+        spread = (along_j + (before + after)) + along_k - 6.0 * middle
+        return 2.0 * middle - fld[1 - p, j + 1, i, lo:hi] + csq[j, i - 1, ks[0]:ks[1]] * spread
+
+    def sample(p, j, ks):
+        i, cells = long // 2 + 1, slice(k0 + ks[0], k0 + ks[1])
+        return later_at(p, j, i, fld[p, j + 1, i - 1, cells], fld[p, j + 1, i, cells], fld[p, j + 1, i + 1, cells], ks)
+
     def advance(p, j, first, count, ks, put, shift=None, sums=None):
         lo, hi = k0 + ks[0], k0 + ks[1]
 
@@ -162,10 +173,7 @@
             before, middle = carry[:2]
             i = first + r + 1
             after = fld[p, j + 1, i + 1, lo:hi]
-            along_j = fld[p, j, i, lo:hi] + fld[p, j + 2, i, lo:hi]
-            along_k = fld[p, j + 1, i, lo - 1:hi - 1] + fld[p, j + 1, i, lo + 1:hi + 1]
-            spread = (along_j + (before + after)) + along_k - 6.0 * middle
-            later = 2.0 * middle - fld[1 - p, j + 1, i, lo:hi] + csq[j, i - 1, ks[0]:ks[1]] * spread
+            later = later_at(p, j, i, before, middle, after, ks)
             put(i - 1, later)
             if sums is None:
                 return middle, after
@@ -253,7 +261,7 @@
         def put(i, later, j=j):
             out[j, i] = later
 
-        shift = fld[p, j + 1, 1, k0:k1]
+        shift = sample(p, j, (0, nk))
         zero = jnp.zeros_like(shift)
         sums = advance(p, j, 0, ni, (0, nk), put, shift, (zero, zero))
         inner_sums[x, 0, j - 1], inner_sums[x, 1, j - 1] = local_sums(*sums, shift)
@@ -274,23 +282,29 @@
 
     for q in range(tiles):
         ks = (q * TILE, (q + 1) * TILE)
-        shifts = [fld[p, j + 1, 1, k0 + ks[0]:k0 + ks[1]] for j in (0, nj - 1)]
-        acc[...] = jnp.zeros_like(acc)
-
         pieces = SPANS if q == tiles - 1 else 1
         count = ni // pieces
 
-        def span(h, q=q, ks=ks, shifts=shifts, pieces=pieces, count=count):
+        def span(h, q=q, ks=ks, pieces=pieces, count=count):
             each_side("py", lambda side: last_plane(q, h if pieces > 1 else None, 1 - side).wait_recv())
+
+            @pl.when(h == 0)
+            def _():
+                for f, j in enumerate((0, nj - 1)):
+                    acc[f, 0] = jnp.zeros(acc.shape[2:], jnp.float32)
+                    acc[f, 1] = jnp.zeros(acc.shape[2:], jnp.float32)
+                    acc[f, 2] = sample(p, j, ks)
+
             for f, j in enumerate((0, nj - 1)):
                 def put(i, later, j=j):
                     out[j, i, ks[0]:ks[1]] = later
 
-                acc[f, 0], acc[f, 1] = advance(p, j, h * count, count, ks, put, shifts[f], (acc[f, 0], acc[f, 1]))
+                sums = advance(p, j, h * count, count, ks, put, acc[f, 2], (acc[f, 0], acc[f, 1]))
+                acc[f, 0], acc[f, 1] = sums
 
         repeat(pieces, span)
         for f in range(2):
-            face_sums[q, x, 0, f], face_sums[q, x, 1, f] = local_sums(acc[f, 0], acc[f, 1], shifts[f])
+            face_sums[q, x, 0, f], face_sums[q, x, 1, f] = local_sums(acc[f, 0], acc[f, 1], acc[f, 2])
         share(face_sums.at[q], q)
         if q == 0:
             settle_inner()
@@ -311,7 +325,10 @@
     nj, ni = f_ref.shape[:2]
     rows = ni // PARTS
     end = pltpu.make_async_copy(f_ref, end_hbm, sems.at[0])
-    end.start()
+    for j in range(nj):
+        for m in range(8):
+            piece = pl.ds(m * (ni // 8), ni // 8)
+            pltpu.make_async_copy(f_ref.at[j, piece], end_hbm.at[j, piece], sems.at[0]).start()
 
     def chunk(m, _):
         for j in range(nj):
@@ -348,7 +365,7 @@
             scratch_shapes=[
                 pltpu.VMEM((2, nj + 2, ni + 2, nk + 2 * PAD, nl), f32),
                 pltpu.VMEM((nj, ni, nk, nl), f32),
-                pltpu.VMEM((2, 2, TILE, nl), f32),
+                pltpu.VMEM((2, 3, TILE, nl), f32),
                 pltpu.VMEM((npx, 2, nj - 2, nk, nl), f32),
                 pltpu.VMEM((nk // TILE, npx, 2, 2, TILE, nl), f32),
                 dma((2, 2)), dma((2, 2, CHUNKS)),

time: 198 us -> 197 us (level)
  no operation moved by 1% of the time
where the time goes in v4:
time: 197 us
  Pallas kernels  197 us (100%)
    pallas_call x1, Pallas kernels, shards(): pl.pallas_call(functools.partial(leapfrog, (nj, ni, nk, npy, npx, npz)),...  191 us
    pallas_call x1, Pallas kernels, shards(): pl.pallas_call(normalise, out_shape=(jax.ShapeDtypeStruct((nj, ni, nk, nl...  5.82 us

profile of v4, /device:TPU:0, one launch (start us, length us, event | category | flops | bytes accessed | tf_op | source)
XLA Modules:
  0.0 197.3 jit_solution(17113974645616400106)
XLA Ops:
  0.6 190.9 %leapfrog.1 = (f32[4,128,32,128]{3,2,1,0:T(8,128)S(1)}, f32[2,4,32,128]{3,2,1,0:T(8,128)S(1)}) custom-call(f32[4,128,32,128]{3,2,1,0:T(8,128)} %f_hbm.1, f32[4,128,32,128]{3,2,1,0:T(8,128)} %e_hbm.1, f32[4,128,32,128]{3,2,1,0:T(8,128)} %c_hbm.1), custom_call_target="tpu_custom_call" | custom-call | tf_op jit(solution)/shard_map/leapfrog/pallas_call | solution.py:360
  191.5 5.8 %normalise.1 = (f32[4,128,32,128]{3,2,1,0:T(8,128)}, f32[4,128,32,128]{3,2,1,0:T(8,128)}) custom-call(f32[4,128,32,128]{3,2,1,0:T(8,128)S(1)} %get-tuple-element.4.f_ref, f32[2,4,32,128]{3,2,1,0:T(8,128)S(1)} %get-tuple-element.5.stat_ref), custom_call_target="tpu_custom_call" | custom-call | tf_op jit(solution)/shard_map/normalise/pallas_call | solution.py:383

commit v5 on v4

--- a/solution.py
+++ b/solution.py
@@ -182,6 +182,28 @@
 
         carry = (fld[p, j + 1, first, lo:hi], fld[p, j + 1, first + 1, lo:hi]) + (sums or ())
         return lax.fori_loop(0, count, row, carry, unroll=4)[2:]
+
+    def advance_faces(p, first, count, ks):
+        faces, cells = (0, nj - 1), slice(k0 + ks[0], k0 + ks[1])
+        shifts = [acc[f, 2] for f in range(2)]
+
+        def row(r, carry):
+            i = first + r + 1
+            left = []
+            for f, j in enumerate(faces):
+                before, middle, total, squares = carry[4 * f:4 * f + 4]
+                after = fld[p, j + 1, i + 1, cells]
+                later = later_at(p, j, i, before, middle, after, ks)
+                out[j, i - 1, ks[0]:ks[1]] = later
+                moved = later - shifts[f]
+                left += [middle, after, total + moved, squares + moved * moved]
+            return tuple(left)
+
+        carry = ()
+        for f, j in enumerate(faces):
+            carry += (fld[p, j + 1, first, cells], fld[p, j + 1, first + 1, cells], acc[f, 0], acc[f, 1])
+        carry = lax.fori_loop(0, count, row, carry, unroll=8)
+        return carry[2:4], carry[6:8]
 
     def with_edges(m, do):
         for side, at in ((0, 0), (1, CHUNKS - 1)):
@@ -295,11 +317,7 @@
                     acc[f, 1] = jnp.zeros(acc.shape[2:], jnp.float32)
                     acc[f, 2] = sample(p, j, ks)
 
-            for f, j in enumerate((0, nj - 1)):
-                def put(i, later, j=j):
-                    out[j, i, ks[0]:ks[1]] = later
-
-                sums = advance(p, j, h * count, count, ks, put, acc[f, 2], (acc[f, 0], acc[f, 1]))
+            for f, sums in enumerate(advance_faces(p, h * count, count, ks)):
                 acc[f, 0], acc[f, 1] = sums
 
         repeat(pieces, span)

time: 197 us -> 197 us (level)
  no operation moved by 1% of the time
where the time goes in v5:
time: 197 us
  Pallas kernels  197 us (100%)
    pallas_call x1, Pallas kernels, shards(): pl.pallas_call(functools.partial(leapfrog, (nj, ni, nk, npy, npx, npz)),...  191 us
    pallas_call x1, Pallas kernels, shards(): pl.pallas_call(normalise, out_shape=(jax.ShapeDtypeStruct((nj, ni, nk, nl...  5.82 us

profile of v5, /device:TPU:0, one launch (start us, length us, event | category | flops | bytes accessed | tf_op | source)
XLA Modules:
  0.0 197.2 jit_solution(596409963478155222)
XLA Ops:
  0.6 190.7 %leapfrog.1 = (f32[4,128,32,128]{3,2,1,0:T(8,128)S(1)}, f32[2,4,32,128]{3,2,1,0:T(8,128)S(1)}) custom-call(f32[4,128,32,128]{3,2,1,0:T(8,128)} %f_hbm.1, f32[4,128,32,128]{3,2,1,0:T(8,128)} %e_hbm.1, f32[4,128,32,128]{3,2,1,0:T(8,128)} %c_hbm.1), custom_call_target="tpu_custom_call" | custom-call | tf_op jit(solution)/shard_map/leapfrog/pallas_call | solution.py:378
  191.4 5.8 %normalise.1 = (f32[4,128,32,128]{3,2,1,0:T(8,128)}, f32[4,128,32,128]{3,2,1,0:T(8,128)}) custom-call(f32[4,128,32,128]{3,2,1,0:T(8,128)S(1)} %get-tuple-element.4.f_ref, f32[2,4,32,128]{3,2,1,0:T(8,128)S(1)} %get-tuple-element.5.stat_ref), custom_call_target="tpu_custom_call" | custom-call | tf_op jit(solution)/shard_map/normalise/pallas_call | solution.py:401
